TPU v7x, 32 devices: a whole 2x2x4 slice. The times are simulated.
32 devices in a mesh: dp: 8 (over z, y), tensor: 4 (over x, core).
Axes of the slice: x: 2, y: 2, z: 4, core: 2. Of those that a mesh axis runs over, the one named last changes fastest.
Arguments:
- out_grad: bfloat16 [2048, 1024], P('dp'), may hold values from -0.29882812 to 0.29882812
- hidden: bfloat16 [2048, 28672], P('dp', 'tensor'), may hold values from -60 to 60
- momentum: float32 [1024, 28672], P('dp', 'tensor'), may hold values from -48 to 48
- second: float32 [1024], P('dp'), may hold values from 0.01 to 0.2
Outputs:
- update: bfloat16 [1024, 28672], P('dp', 'tensor')
- momentum_out: float32 [1024, 28672], P('dp', 'tensor')
- second_out: float32 [1024], P('dp')
All inputs are finite; a program needn't handle non-finite values.
Results may differ from a plain program's by a relative error of at most 0.035.
Values may be sent and summed in bfloat16 or wider, within the bound.
A program may use at most 128 MiB of HBM per device.

v0:
```python
import jax
import jax.numpy as jnp
from jax import lax
from jax.sharding import PartitionSpec as P

FF = 28672
ITERS = 3


quintic_a = 3.4445
quintic_b = -4.775
quintic_c = 2.0315
beta_one = 0.95
beta_two = 0.95


def summed_gram(partial_gram):
    return lax.psum(partial_gram.astype(jnp.bfloat16), "tensor").astype(jnp.float32)


def newton_schulz(current, reduce_gram):
    for iteration in range(ITERS):
        gram = reduce_gram(jnp.dot(current, current.T, preferred_element_type=jnp.float32)).astype(
            jnp.bfloat16
        )
        square = jnp.dot(gram, gram, preferred_element_type=jnp.float32)
        poly = (quintic_b * gram.astype(jnp.float32) + quintic_c * square).astype(jnp.bfloat16)
        current = (
            quintic_a * current.astype(jnp.float32)
            + jnp.dot(poly, current, preferred_element_type=jnp.float32)
        ).astype(jnp.bfloat16)
    return current


def body(out_grad, hidden, momentum, second):
    grad = lax.psum_scatter(
        lax.dot_general(
            out_grad, hidden, (((0,), (0,)), ((), ())), preferred_element_type=jnp.float32
        ).astype(jnp.bfloat16),
        "dp",
        scatter_dimension=0,
        tiled=True,
    ).astype(jnp.float32)
    momentum_out = beta_one * momentum + grad
    nesterov = grad + beta_one * momentum_out
    norm_sum = lax.psum(jnp.sum(nesterov * nesterov), "tensor")
    start_panel = (nesterov / (jnp.sqrt(norm_sum) + 1e-07)).astype(jnp.bfloat16)
    orthogonal = newton_schulz(start_panel, summed_gram)
    local_wide = orthogonal.astype(jnp.float32)
    energy = lax.psum(jnp.sum(local_wide * local_wide, axis=1), "tensor")
    second_out = beta_two * second + (1.0 - beta_two) * energy
    update = (orthogonal.astype(jnp.float32) * jnp.sqrt(FF / second_out)[:, None]).astype(
        jnp.bfloat16
    )
    return (update, momentum_out, second_out)


def solution(mesh):
    placed = (P("dp", None), P("dp", "tensor"), P("dp", "tensor"), P("dp"))
    return jax.shard_map(
        body,
        mesh=mesh,
        in_specs=placed,
        out_specs=(P("dp", "tensor"), P("dp", "tensor"), P("dp")),
        check_vma=False,
    )
```

profile of v0, /device:TPU:1, one launch (start us, length us, event | category | flops | bytes accessed | tf_op | source)
XLA Modules:
  0.0 333.6 jit_solution(9112462617229319903)
XLA Ops:
  7.2 0.0 copy-start
  7.2 0.0 reduce-scatter.2.cloned.1.call-start
  7.2 1.0 copy-done
  8.2 9.4 %convolution_convert_fusion = bf16[1024,7168]{1,0:T(8,128)(2,1)} fusion(bf16[256,1024]{1,0:T(8,128)(2,1)S(1)} %copy-done, bf16[256,7168]{1,0:T(8,128)(2,1)} %param.5), kind=kOutput, calls=%fused_computation | convolution fusion | flops 3765436416 | bytes 18874368 | tf_op jit(solution)/shard_map/dot_general | solution.py:37
  17.6 0.0 reduce-scatter.2.cloned.1.call-update
  17.6 238.8 %reduce-scatter.2.cloned.1.call-done = bf16[128,7168]{1,0:T(8,128)(2,1)} async-done(((bf16[1024,7168]{1,0:T(8,128)(2,1)}), bf16[128,7168]{1,0:T(8,128)(2,1)}) %reduce-scatter.2.cloned.1.call-update) | async-done | bytes 1835024 | tf_op jit(solution)/shard_map/reduce_scatter | solution.py:36
  256.4 6.0 %multiply_reduce_fusion.1 = (f32[]{:T(128)}, f32[128,7168]{1,0:T(8,128)}) fusion(bf16[128,7168]{1,0:T(8,128)(2,1)} %reduce-scatter.2.cloned.1.call-done, f32[128,7168]{1,0:T(8,128)} %param.6), kind=kLoop, calls=%fused_computation.13 | loop fusion | flops 6422527 | bytes 9175044 | tf_op jit(solution)/shard_map/reduce_sum | solution.py:46
  262.5 6.4 %psum.35 = f32[]{:T(128)} all-reduce(f32[]{:T(128)} %get-tuple-element.5), channel_id=1, replica_groups=mesh['dp'=8,'tensor'=4] {'tensor'}, use_global_device_ids=true, to_apply=%region_2.0 | all-reduce | flops 1 | bytes 8 | tf_op jit(solution)/shard_map/psum | solution.py:46
  269.6 2.6 divide_convert_fusion
  272.2 0.0 copy-start.2
  272.2 1.2 copy-done.2
  273.4 0.6 convolution_convert_fusion.3
  274.0 10.9 %psum.36 = bf16[128,128]{1,0:T(8,128)(2,1)S(1)} all-reduce(bf16[128,128]{1,0:T(8,128)(2,1)S(1)} %convolution_convert_fusion.3), channel_id=1, replica_groups=mesh['dp'=8,'tensor'=4] {'tensor'}, use_global_device_ids=true, to_apply=%region_3.0 | all-reduce | flops 16384 | bytes 65536 | tf_op jit(solution)/shard_map/psum | solution.py:18
  285.0 2.8 fusion
  287.8 0.6 convolution_convert_fusion.2
  288.5 10.3 %psum.37 = bf16[128,128]{1,0:T(8,128)(2,1)S(1)} all-reduce(bf16[128,128]{1,0:T(8,128)(2,1)S(1)} %convolution_convert_fusion.2), channel_id=1, replica_groups=mesh['dp'=8,'tensor'=4] {'tensor'}, use_global_device_ids=true, to_apply=%region_4.0 | all-reduce | flops 16384 | bytes 65536 | tf_op jit(solution)/shard_map/psum | solution.py:18
  298.8 2.0 fusion.1
  300.8 2.8 convolution_convert_fusion.1
  303.6 0.0 copy-start.4
  303.6 10.4 %psum.38 = bf16[128,128]{1,0:T(8,128)(2,1)S(1)} all-reduce(bf16[128,128]{1,0:T(8,128)(2,1)S(1)} %convolution_convert_fusion.1), channel_id=1, replica_groups=mesh['dp'=8,'tensor'=4] {'tensor'}, use_global_device_ids=true, to_apply=%region_5.0 | all-reduce | flops 16384 | bytes 65536 | tf_op jit(solution)/shard_map/psum | solution.py:18
  314.0 2.8 multiply_reduce_fusion
  316.8 5.8 %psum.39 = f32[128]{0:T(128)S(1)} all-reduce(f32[128]{0:T(128)S(1)} %get-tuple-element.7), channel_id=1, replica_groups=mesh['dp'=8,'tensor'=4] {'tensor'}, use_global_device_ids=true, to_apply=%region_7.0 | all-reduce | flops 128 | bytes 1024 | tf_op jit(solution)/shard_map/psum | solution.py:50
  322.6 0.5 divide_sqrt_fusion
  323.1 3.6 %multiply_convert_fusion = bf16[128,7168]{1,0:T(8,128)(2,1)} fusion(f32[128,7168]{1,0:T(8,128)} %get-tuple-element.8, f32[128]{0:T(128)S(1)} %get-tuple-element.3), kind=kLoop, calls=%fused_computation.10 | loop fusion | flops 1835008 | bytes 5505536 | tf_op jit(solution)/shard_map/convert_element_type | solution.py:52
  (5 shorter events, 0.0 us)
Async XLA Ops:
  7.2 1.0 copy-start
  7.2 249.3 %reduce-scatter.2.cloned.1.call-start = ((), (), s32[]{:S(2)}) async-start(), calls=%async_computation.1 | async-start | bytes 16515072 | tf_op jit(solution)/shard_map/reduce_scatter | solution.py:36
  256.4 13.1 %copy-start.3 = (bf16[128,7168]{1,0:T(8,128)(2,1)S(1)}, bf16[128,7168]{1,0:T(8,128)(2,1)}, u32[]{:S(2)}) copy-start(bf16[128,7168]{1,0:T(8,128)(2,1)} %reduce-scatter.2.cloned.1.call-done) | copy-start | bytes 5505028
  272.2 1.2 copy-start.2
  300.8 13.3 %copy-start.1 = (bf16[128,7168]{1,0:T(8,128)(2,1)S(1)}, bf16[128,7168]{1,0:T(8,128)(2,1)}, u32[]{:S(2)}) copy-start(bf16[128,7168]{1,0:T(8,128)(2,1)} %fusion.1) | copy-start | bytes 5505028
  303.6 19.0 %copy-start.4 = (f32[128]{0:T(128)S(1)}, f32[128]{0:T(128)}, u32[]{:S(2)}) copy-start(f32[128]{0:T(128)} %param.7) | copy-start | bytes 1540
Sparse Core Ops, SparseCore 0:
  17.7 238.6 reduce-scatter.1
where the time goes:
time: 335 us; the launch traced here: 334 us
  waiting for transfers between devices  239 us (71%)
  blocking collectives  43.8 us (13%)
  matrix products  21.1 us (6%)
  between operations  14.8 us (4%)
  other arithmetic  12.7 us (4%)
    reduce_scatter x1, waiting for transfers between devices, body(): lax.psum_scatter(lax.dot_general(out_grad, hidden, (((0,), (0,)), ((), ()...  239 us
    psum x3, blocking collectives, summed_gram(): lax.psum(partial_gram.astype(jnp.bfloat16), 'tensor').astype(jnp.float32)  31.6 us
    dot_general x1, matrix products, body(): lax.dot_general(out_grad, hidden, (((0,), (0,)), ((), ())), preferred_ele...  9.36 us
    dot_general x3, matrix products, newton_schulz(): jnp.dot(poly, current, preferred_element_type=jnp.float32)  7.65 us
  transfers between devices with their start and end apart: 1, of which 1 were waited for; matrix products, arithmetic and copies ran while one was open for 0% of the time, Pallas kernels for 0%

commit v1 on v0

v1 whole, which is shorter than its diff:
```python
import functools

import jax
import jax.numpy as jnp
from jax import lax
from jax.experimental import pallas as pl
from jax.experimental.pallas import tpu as pltpu
from jax.sharding import PartitionSpec as P

ITERS = 3
quintic_a = 3.4445
quintic_b = -4.775
quintic_c = 2.0315
beta_one = 0.95
beta_two = 0.95

MESH = pl.DeviceIdType.MESH
F32 = jnp.float32
BF16 = jnp.bfloat16


def line_split(n_dp):
    ny = 1
    while ny * ny * 4 <= n_dp and n_dp % (ny * 2) == 0:
        ny *= 2
    return n_dp // ny, ny


def exact_dot(a, b):
    return jnp.dot(a, b, preferred_element_type=F32, precision=lax.Precision.HIGHEST)


def kernel(
    nz, ny, nt, n_chunks, ff,
    og_hbm, h_hbm, mom_hbm, sec_ref,
    upd_hbm, momout_hbm, secout_ref,
    h, ograw, og_t, rr, rl, sr, sl, mom, x, gram, norm, g_all,
    h_sem, og_sem, y_send, og_send, rr_sem, rl_sem, sr_sem, sl_sem, mom_sem, momout_sem, upd_sem,
    g_send, g_recv,
):
    tokens = h_hbm.shape[0]
    rows, width = x.shape[1], x.shape[2]
    d = lax.axis_index("dp")
    t = lax.axis_index("tensor")
    z, y = d // ny, lax.rem(d, ny)

    def at_y(k):
        return (z * ny + lax.rem(y + k, ny), t)

    def at_z(step):
        return (d + step * ny, t)

    def at_t(k):
        return (d, lax.rem(t + k, nt))

    barrier = pltpu.get_barrier_semaphore()
    for k in range(1, ny):
        pl.semaphore_signal(barrier, inc=1, device_id=at_y(k), device_id_type=MESH)
    for k in range(1, nt):
        pl.semaphore_signal(barrier, inc=1, device_id=at_t(k), device_id_type=MESH)

    @pl.when(z > 0)
    def _():
        pl.semaphore_signal(barrier, inc=1, device_id=at_z(-1), device_id_type=MESH)

    @pl.when(z < nz - 1)
    def _():
        pl.semaphore_signal(barrier, inc=1, device_id=at_z(1), device_id_type=MESH)

    mine = pl.ds(pl.multiple_of(y * tokens, tokens), tokens)
    for j in range(nz):
        cols = pl.ds(pl.multiple_of((j * ny + y) * rows, rows), rows)
        pltpu.make_async_copy(og_hbm.at[:, cols], ograw.at[y, j], og_sem.at[y]).start()

    def columns(c):
        return pl.ds(pl.multiple_of(c * width, width), width)

    def own_load(c, carry):
        pltpu.make_async_copy(h_hbm.at[:, columns(c)], h.at[c, mine], h_sem.at[y, c]).start()
        return carry

    lax.fori_loop(0, n_chunks, own_load, 0)

    ends = jnp.minimum(z, 1) + jnp.minimum(nz - 1 - z, 1)
    pl.semaphore_wait(barrier, (ny - 1) + (nt - 1) + ends)

    for k in range(1, ny):
        peer = lax.rem(y + k, ny)
        for j in range(nz):
            cols = pl.ds(pl.multiple_of((j * ny + peer) * rows, rows), rows)
            pltpu.make_async_remote_copy(
                og_hbm.at[:, cols], ograw.at[y, j], og_send.at[k - 1], og_sem.at[y],
                device_id=at_y(k), device_id_type=MESH,
            ).start()

    def y_sends(c, carry):
        for k in range(1, ny):
            pltpu.make_async_remote_copy(
                h_hbm.at[:, columns(c)], h.at[c, mine], y_send.at[k - 1], h_sem.at[y, c],
                device_id=at_y(k), device_id_type=MESH,
            ).start()
        return carry

    lax.fori_loop(0, n_chunks, y_sends, 0)

    def mom_load(c, carry):
        pltpu.make_async_copy(mom_hbm.at[:, columns(c)], mom.at[c], mom_sem).start()
        return carry

    lax.fori_loop(0, n_chunks, mom_load, 0)
    gram[...] = jnp.zeros_like(gram)
    norm[...] = jnp.zeros_like(norm)
    for k in range(ny):
        pltpu.make_async_copy(ograw.at[k], ograw.at[k], og_sem.at[k]).wait()
    for k in range(ny):
        for j in range(nz):
            og_t[j, :, k * tokens : (k + 1) * tokens] = ograw[k, j].T
    pltpu.make_async_copy(mom, mom, mom_sem).wait()

    def partial(j, c):
        return jnp.dot(og_t[j], h[c], preferred_element_type=F32)

    def send_on(j, c, slot, first, recv, recv_sem, send, send_sem, step):
        own = partial(j, c)

        @pl.when(first)
        def _():
            send[slot, c] = own.astype(BF16)

        @pl.when(jnp.logical_not(first))
        def _():
            pltpu.make_async_copy(recv.at[slot, c], recv.at[slot, c], recv_sem.at[slot, c]).wait()
            send[slot, c] = (own + recv[slot, c].astype(F32)).astype(BF16)

        pltpu.make_async_remote_copy(
            send.at[slot, c], recv.at[slot, c], send_sem.at[slot], recv_sem.at[slot, c],
            device_id=at_z(step), device_id_type=MESH,
        ).start()

    reach = jnp.maximum(z, nz - 1 - z)

    def step(s, carry):
        @pl.when(s < n_chunks)
        def _():
            for k in range(ny):
                block = h.at[s, pl.ds(k * tokens, tokens)]
                pltpu.make_async_copy(block, block, h_sem.at[k, s]).wait()

        right = s - z

        @pl.when(jnp.logical_and(right >= 0, right < n_chunks))
        def _():
            for j in range(nz - 1, 0, -1):
                @pl.when(z < j)
                def _():
                    send_on(j, right, j - 1, z == 0, rr, rr_sem, sr, sr_sem, 1)

        left = s - (nz - 1 - z)

        @pl.when(jnp.logical_and(left >= 0, left < n_chunks))
        def _():
            for j in range(nz - 1):
                @pl.when(z > j)
                def _():
                    send_on(j, left, j, z == nz - 1, rl, rl_sem, sl, sl_sem, -1)

        c = s - reach

        @pl.when(jnp.logical_and(c >= 0, c < n_chunks))
        def _():
            x_grad = norm.at[1]
            x_grad[...] = partial(z, c)

            @pl.when(z > 0)
            def _():
                pltpu.make_async_copy(rr.at[z - 1, c], rr.at[z - 1, c], rr_sem.at[z - 1, c]).wait()
                x_grad[...] += rr[z - 1, c].astype(F32)

            @pl.when(z < nz - 1)
            def _():
                pltpu.make_async_copy(rl.at[z, c], rl.at[z, c], rl_sem.at[z, c]).wait()
                x_grad[...] += rl[z, c].astype(F32)

            grad = x_grad[...]
            momentum_out = beta_one * mom[c] + grad
            nesterov = grad + beta_one * momentum_out
            mom[c] = momentum_out
            pltpu.make_async_copy(mom.at[c], momout_hbm.at[:, columns(c)], momout_sem).start()
            panel = nesterov.astype(BF16)
            x[c] = panel
            norm[0] += nesterov * nesterov
            gram[...] += lax.dot_general(
                panel, panel, (((1,), (1,)), ((), ())), preferred_element_type=F32
            )

        return carry

    lax.fori_loop(0, n_chunks + nz - 1, step, 0)

    g_all[t, :rows] = gram[...]
    total = jnp.sum(jnp.sum(norm[0], axis=0, keepdims=True), axis=1, keepdims=True)
    g_all[t, rows:] = jnp.broadcast_to(total, (8, rows))
    for k in range(1, nt):
        pltpu.make_async_remote_copy(
            g_all.at[t], g_all.at[t], g_send.at[k - 1], g_recv.at[t],
            device_id=at_t(k), device_id_type=MESH,
        ).start()
    for k in range(nt):
        @pl.when(k != t)
        def _():
            pltpu.make_async_copy(g_all.at[k], g_all.at[k], g_recv.at[k]).wait()
    summed = g_all[0]
    for k in range(1, nt):
        summed = summed + g_all[k]
    inverse = 1.0 / (jnp.sqrt(summed[rows : rows + 1]) + 1e-07)
    current = summed[:rows] * inverse * inverse
    eye = (
        lax.broadcasted_iota(jnp.int32, (rows, rows), 0)
        == lax.broadcasted_iota(jnp.int32, (rows, rows), 1)
    ).astype(F32)
    map_all = None
    for _ in range(ITERS):
        square = exact_dot(current, current)
        map_one = quintic_a * eye + quintic_b * current + quintic_c * square
        map_all = map_one if map_all is None else exact_dot(map_one, map_all)
        current = exact_dot(map_one, exact_dot(current, map_one))
    energy = jnp.sum(current * eye, axis=0, keepdims=True)
    second_out = beta_two * sec_ref[...] + (1.0 - beta_two) * energy
    secout_ref[...] = second_out
    scale = jnp.sqrt(ff / second_out) * inverse
    final = jnp.sum(eye * scale, axis=1, keepdims=True) * map_all
    high = final.astype(BF16)
    low = (final - high.astype(F32)).astype(BF16)

    def finish(c, carry):
        panel = x[c]
        out = jnp.dot(high, panel, preferred_element_type=F32)
        out += jnp.dot(low, panel, preferred_element_type=F32)
        x[c] = out.astype(BF16)
        pltpu.make_async_copy(x.at[c], upd_hbm.at[:, columns(c)], upd_sem).start()
        return carry

    lax.fori_loop(0, n_chunks, finish, 0)

    pltpu.make_async_copy(mom, mom, momout_sem).wait()
    for k in range(1, ny):
        pltpu.make_async_copy(ograw.at[0], ograw.at[0], og_send.at[k - 1]).wait()
        blocks = h.at[:, pl.ds(0, tokens)]
        pltpu.make_async_copy(blocks, blocks, y_send.at[k - 1]).wait()
    for j in range(1, nz):
        @pl.when(z < j)
        def _():
            pltpu.make_async_copy(sr.at[j - 1], sr.at[j - 1], sr_sem.at[j - 1]).wait()
    for j in range(nz - 1):
        @pl.when(z > j)
        def _():
            pltpu.make_async_copy(sl.at[j], sl.at[j], sl_sem.at[j]).wait()
    for k in range(1, nt):
        pltpu.make_async_copy(g_all.at[0], g_all.at[0], g_send.at[k - 1]).wait()
    pltpu.make_async_copy(x, x, upd_sem).wait()


def body(nz, ny, nt, out_grad, hidden, momentum, second):
    tokens, cols = hidden.shape
    rows = momentum.shape[0]
    width = 256 if cols % 256 == 0 else 128
    n_chunks = cols // width
    dma = pltpu.SemaphoreType.DMA
    anywhere = pl.BlockSpec(memory_space=pl.ANY)
    vmem = pl.BlockSpec(memory_space=pltpu.VMEM)
    hops = (nz - 1, n_chunks)
    update, momentum_out, second_out = pl.pallas_call(
        functools.partial(kernel, nz, ny, nt, n_chunks, float(cols * nt)),
        out_shape=(
            jax.ShapeDtypeStruct((rows, cols), BF16),
            jax.ShapeDtypeStruct((rows, cols), F32),
            jax.ShapeDtypeStruct((1, rows), F32),
        ),
        in_specs=[anywhere, anywhere, anywhere, vmem],
        out_specs=(anywhere, anywhere, vmem),
        scratch_shapes=[
            pltpu.VMEM((n_chunks, ny * tokens, width), BF16),
            pltpu.VMEM((ny, nz, tokens, rows), BF16),
            pltpu.VMEM((nz, rows, ny * tokens), BF16),
            pltpu.VMEM(hops + (rows, width), BF16),
            pltpu.VMEM(hops + (rows, width), BF16),
            pltpu.VMEM(hops + (rows, width), BF16),
            pltpu.VMEM(hops + (rows, width), BF16),
            pltpu.VMEM((n_chunks, rows, width), F32),
            pltpu.VMEM((n_chunks, rows, width), BF16),
            pltpu.VMEM((rows, rows), F32),
            pltpu.VMEM((2, rows, width), F32),
            pltpu.VMEM((nt, rows + 8, rows), F32),
            dma((ny, n_chunks)),
            dma((ny,)),
            dma((max(ny - 1, 1),)),
            dma((max(ny - 1, 1),)),
            dma(hops),
            dma(hops),
            dma((nz - 1,)),
            dma((nz - 1,)),
            dma,
            dma,
            dma,
            dma((max(nt - 1, 1),)),
            dma((nt,)),
        ],
        compiler_params=pltpu.CompilerParams(
            collective_id=0, has_side_effects=True, vmem_limit_bytes=60 * 1024 * 1024
        ),
        name="normuon",
    )(out_grad, hidden, momentum, second.reshape(1, rows))
    return update, momentum_out, second_out.reshape(rows)


def solution(mesh):
    nz, ny = line_split(mesh.shape["dp"])
    placed = (P("dp", None), P("dp", "tensor"), P("dp", "tensor"), P("dp"))
    return jax.shard_map(
        functools.partial(body, nz, ny, mesh.shape["tensor"]),
        mesh=mesh,
        in_specs=placed,
        out_specs=(P("dp", "tensor"), P("dp", "tensor"), P("dp")),
        check_vma=False,
    )
```

time: 335 us -> 161 us (0.48)
  waiting for transfers between devices: 239 us -> 0 us
  Pallas kernels: 0 us -> 155 us
  blocking collectives: 43.8 us -> 0 us
  matrix products: 21.1 us -> 0 us
  between operations: 14.8 us -> 0.65 us
  other arithmetic: 12.7 us -> 0 us
    reduce_scatter x1 -> x0, waiting for transfers between devices: 239 us -> none  [body(): lax.psum_scatter(lax.dot_general(out_grad, hidden, (((0,), (0,)), ((), ()...]
    pallas_call x0 -> x1, Pallas kernels: none -> 155 us  [body(): pl.pallas_call(functools.partial(kernel, nz, ny, nt, n_chunks, float(cols...]
    psum x5 -> x0, blocking collectives: 43.8 us -> none  [the longest x3 31.6 us: summed_gram(): lax.psum(partial_gram.astype(jnp.bfloat16), 'tensor').astype(jnp.float32)]
    dot_general x7 -> x0, matrix products: 21.1 us -> none  [the longest x1 9.36 us: body(): lax.dot_general(out_grad, hidden, (((0,), (0,)), ((), ())), preferred_ele...]
    convert_element_type x2 -> x0, other arithmetic: 6.16 us -> none  [the longest x1 3.58 us: body(): (orthogonal.astype(jnp.float32) * jnp.sqrt(FF / second_out)[:, None]).ast...]
    reduce_sum x1 -> x0, other arithmetic: 6.05 us -> none  [body(): norm_sum = lax.psum(jnp.sum(nesterov * nesterov), 'tensor')]
  transfers between devices with their start and end apart: 1 -> 0, of which waited for: 1 -> 0; matrix products, arithmetic and copies ran while one was open for 0% -> 0% of each run, Pallas kernels for 0% -> 0%
where the time goes in v1:
time: 161 us
  Pallas kernels  155 us (96%)
  local copies, waits for them, and re-layouts  5.35 us (3%)
    pallas_call x1, Pallas kernels, body(): pl.pallas_call(functools.partial(kernel, nz, ny, nt, n_chunks, float(cols...  155 us
    unnamed x7, local copies, waits for them, and re-layouts  5.35 us

profile of v1, /device:TPU:1, one launch (start us, length us, event | category | flops | bytes accessed | tf_op | source)
XLA Modules:
  0.0 160.8 jit_solution(6437503087022624874)
XLA Ops:
  0.6 154.8 %normuon.1 = (bf16[128,7168]{1,0:T(8,128)(2,1)}, f32[128,7168]{1,0:T(8,128)}, f32[1,128]{1,0:T(1,128)}) custom-call(bf16[256,1024]{1,0:T(8,128)(2,1)} %og_hbm.1, bf16[256,7168]{1,0:T(8,128)(2,1)} %h_hbm.1, f32[128,7168]{1,0:T(8,128)} %mom_hbm.1, f32[1,128]{1,0:T(1,128)} %bitcast.2), custom_call_target="tpu_custom_call" | custom-call | tf_op jit(solution)/shard_map/normuon/pallas_call | solution.py:272
  155.4 0.0 copy-start
  155.4 3.0 %copy.10 = bf16[128,7168]{1,0:T(8,128)(2,1)} copy(bf16[128,7168]{1,0:T(8,128)(2,1)} %get-tuple-element.12) | data formatting | bytes 3670016
  158.4 0.0 copy-done
  158.4 0.0 copy-start.1
  158.4 1.8 %copy.11 = f32[128,7168]{1,0:T(8,128)} copy(f32[128,7168]{1,0:T(8,128)S(1)} %copy-done) | data formatting | bytes 7340032
  160.3 0.0 copy-done.1
  160.3 0.5 copy.12
Async XLA Ops:
  155.4 3.0 %copy-start = (f32[128,7168]{1,0:T(8,128)S(1)}, f32[128,7168]{1,0:T(8,128)}, u32[]{:S(2)}) copy-start(f32[128,7168]{1,0:T(8,128)} %get-tuple-element.13) | copy-start | bytes 11010052
  158.4 1.8 %copy-start.1 = (f32[1,128]{1,0:T(1,128)S(1)}, f32[1,128]{1,0:T(1,128)}, u32[]{:S(2)}) copy-start(f32[1,128]{1,0:T(1,128)} %get-tuple-element.8) | copy-start | bytes 1540

commit v2 on v1

--- a/solution.py
+++ b/solution.py
@@ -33,9 +33,9 @@
 def kernel(
     nz, ny, nt, n_chunks, ff,
     og_hbm, h_hbm, mom_hbm, sec_ref,
-    upd_hbm, momout_hbm, secout_ref,
-    h, ograw, og_t, rr, rl, sr, sl, mom, x, gram, norm, g_all,
-    h_sem, og_sem, y_send, og_send, rr_sem, rl_sem, sr_sem, sl_sem, mom_sem, momout_sem, upd_sem,
+    x, mom, final_ref, secout_ref,
+    h, ograw, og_t, rr, rl, sr, sl, gram, norm, g_all,
+    h_sem, og_sem, y_send, og_send, rr_sem, rl_sem, sr_sem, sl_sem, mom_sem,
     g_send, g_recv,
 ):
     tokens = h_hbm.shape[0]
@@ -68,28 +68,23 @@
         pl.semaphore_signal(barrier, inc=1, device_id=at_z(1), device_id_type=MESH)
 
     mine = pl.ds(pl.multiple_of(y * tokens, tokens), tokens)
-    for j in range(nz):
-        cols = pl.ds(pl.multiple_of((j * ny + y) * rows, rows), rows)
-        pltpu.make_async_copy(og_hbm.at[:, cols], ograw.at[y, j], og_sem.at[y]).start()
 
     def columns(c):
         return pl.ds(pl.multiple_of(c * width, width), width)
 
-    def own_load(c, carry):
-        pltpu.make_async_copy(h_hbm.at[:, columns(c)], h.at[c, mine], h_sem.at[y, c]).start()
-        return carry
-
-    lax.fori_loop(0, n_chunks, own_load, 0)
-
     ends = jnp.minimum(z, 1) + jnp.minimum(nz - 1 - z, 1)
     pl.semaphore_wait(barrier, (ny - 1) + (nt - 1) + ends)
 
-    for k in range(1, ny):
-        peer = lax.rem(y + k, ny)
-        for j in range(nz):
+    def far_first(i):
+        return jnp.where(z * 2 < nz, nz - 1 - i, i)
+
+    def og_sends(i):
+        j = far_first(i)
+        for k in range(1, ny):
+            peer = lax.rem(y + k, ny)
             cols = pl.ds(pl.multiple_of((j * ny + peer) * rows, rows), rows)
             pltpu.make_async_remote_copy(
-                og_hbm.at[:, cols], ograw.at[y, j], og_send.at[k - 1], og_sem.at[y],
+                og_hbm.at[:, cols], ograw.at[y, j], og_send.at[k - 1], og_sem.at[y, j],
                 device_id=at_y(k), device_id_type=MESH,
             ).start()
 
@@ -101,7 +96,21 @@
             ).start()
         return carry
 
-    lax.fori_loop(0, n_chunks, y_sends, 0)
+    og_sends(0)
+    y_sends(0, 0)
+    for i in range(1, nz):
+        og_sends(i)
+    lax.fori_loop(1, n_chunks, y_sends, 0)
+
+    for j in range(nz):
+        cols = pl.ds(pl.multiple_of((j * ny + y) * rows, rows), rows)
+        pltpu.make_async_copy(og_hbm.at[:, cols], ograw.at[y, j], og_sem.at[y, j]).start()
+
+    def own_load(c, carry):
+        pltpu.make_async_copy(h_hbm.at[:, columns(c)], h.at[c, mine], h_sem.at[y, c]).start()
+        return carry
+
+    lax.fori_loop(0, n_chunks, own_load, 0)
 
     def mom_load(c, carry):
         pltpu.make_async_copy(mom_hbm.at[:, columns(c)], mom.at[c], mom_sem).start()
@@ -110,12 +119,12 @@
     lax.fori_loop(0, n_chunks, mom_load, 0)
     gram[...] = jnp.zeros_like(gram)
     norm[...] = jnp.zeros_like(norm)
-    for k in range(ny):
-        pltpu.make_async_copy(ograw.at[k], ograw.at[k], og_sem.at[k]).wait()
-    for k in range(ny):
-        for j in range(nz):
+    pltpu.make_async_copy(mom, mom, mom_sem).wait()
+
+    def prepare(j):
+        for k in range(ny):
+            pltpu.make_async_copy(ograw.at[k, j], ograw.at[k, j], og_sem.at[k, j]).wait()
             og_t[j, :, k * tokens : (k + 1) * tokens] = ograw[k, j].T
-    pltpu.make_async_copy(mom, mom, mom_sem).wait()
 
     def partial(j, c):
         return jnp.dot(og_t[j], h[c], preferred_element_type=F32)
@@ -153,6 +162,10 @@
             for j in range(nz - 1, 0, -1):
                 @pl.when(z < j)
                 def _():
+                    @pl.when(s == 0)
+                    def _():
+                        prepare(j)
+
                     send_on(j, right, j - 1, z == 0, rr, rr_sem, sr, sr_sem, 1)
 
         left = s - (nz - 1 - z)
@@ -162,7 +175,18 @@
             for j in range(nz - 1):
                 @pl.when(z > j)
                 def _():
+                    @pl.when(s == 0)
+                    def _():
+                        prepare(j)
+
                     send_on(j, left, j, z == nz - 1, rl, rl_sem, sl, sl_sem, -1)
+
+        for j in range(nz):
+            inner = jnp.logical_and(z > 0, z < nz - 1)
+
+            @pl.when(jnp.logical_and(s == 0, jnp.logical_or(inner, z == j)))
+            def _():
+                prepare(j)
 
         c = s - reach
 
@@ -185,7 +209,6 @@
             momentum_out = beta_one * mom[c] + grad
             nesterov = grad + beta_one * momentum_out
             mom[c] = momentum_out
-            pltpu.make_async_copy(mom.at[c], momout_hbm.at[:, columns(c)], momout_sem).start()
             panel = nesterov.astype(BF16)
             x[c] = panel
             norm[0] += nesterov * nesterov
@@ -219,30 +242,20 @@
         == lax.broadcasted_iota(jnp.int32, (rows, rows), 1)
     ).astype(F32)
     map_all = None
-    for _ in range(ITERS):
+    for iteration in range(ITERS):
         square = exact_dot(current, current)
         map_one = quintic_a * eye + quintic_b * current + quintic_c * square
         map_all = map_one if map_all is None else exact_dot(map_one, map_all)
-        current = exact_dot(map_one, exact_dot(current, map_one))
-    energy = jnp.sum(current * eye, axis=0, keepdims=True)
+        mapped = exact_dot(map_one, current)
+        if iteration < ITERS - 1:
+            current = exact_dot(mapped, map_one)
+    energy = jnp.sum(mapped * map_one, axis=0, keepdims=True)
     second_out = beta_two * sec_ref[...] + (1.0 - beta_two) * energy
     secout_ref[...] = second_out
     scale = jnp.sqrt(ff / second_out) * inverse
     final = jnp.sum(eye * scale, axis=1, keepdims=True) * map_all
-    high = final.astype(BF16)
-    low = (final - high.astype(F32)).astype(BF16)
-
-    def finish(c, carry):
-        panel = x[c]
-        out = jnp.dot(high, panel, preferred_element_type=F32)
-        out += jnp.dot(low, panel, preferred_element_type=F32)
-        x[c] = out.astype(BF16)
-        pltpu.make_async_copy(x.at[c], upd_hbm.at[:, columns(c)], upd_sem).start()
-        return carry
-
-    lax.fori_loop(0, n_chunks, finish, 0)
-
-    pltpu.make_async_copy(mom, mom, momout_sem).wait()
+    final_ref[...] = final
+
     for k in range(1, ny):
         pltpu.make_async_copy(ograw.at[0], ograw.at[0], og_send.at[k - 1]).wait()
         blocks = h.at[:, pl.ds(0, tokens)]
@@ -257,7 +270,30 @@
             pltpu.make_async_copy(sl.at[j], sl.at[j], sl_sem.at[j]).wait()
     for k in range(1, nt):
         pltpu.make_async_copy(g_all.at[0], g_all.at[0], g_send.at[k - 1]).wait()
-    pltpu.make_async_copy(x, x, upd_sem).wait()
+
+
+def write_kernel(n_chunks, x, mom, final_ref, sec_ref, upd_hbm, momout_hbm, secout_ref, out, mom_sem, upd_sem):
+    width = x.shape[2]
+
+    def columns(c):
+        return pl.ds(pl.multiple_of(c * width, width), width)
+
+    high = final_ref[...].astype(BF16)
+    low = (final_ref[...] - high.astype(F32)).astype(BF16)
+    secout_ref[...] = sec_ref[...]
+
+    def finish(c, carry):
+        pltpu.make_async_copy(mom.at[c], momout_hbm.at[:, columns(c)], mom_sem).start()
+        panel = x[c]
+        result = jnp.dot(high, panel, preferred_element_type=F32)
+        result += jnp.dot(low, panel, preferred_element_type=F32)
+        out[c] = result.astype(BF16)
+        pltpu.make_async_copy(out.at[c], upd_hbm.at[:, columns(c)], upd_sem).start()
+        return carry
+
+    lax.fori_loop(0, n_chunks, finish, 0)
+    pltpu.make_async_copy(mom, mom, mom_sem).wait()
+    pltpu.make_async_copy(out, out, upd_sem).wait()
 
 
 def body(nz, ny, nt, out_grad, hidden, momentum, second):
@@ -266,18 +302,19 @@
     width = 256 if cols % 256 == 0 else 128
     n_chunks = cols // width
     dma = pltpu.SemaphoreType.DMA
-    anywhere = pl.BlockSpec(memory_space=pl.ANY)
+    anywhere = pl.BlockSpec(memory_space=pltpu.HBM)
     vmem = pl.BlockSpec(memory_space=pltpu.VMEM)
     hops = (nz - 1, n_chunks)
-    update, momentum_out, second_out = pl.pallas_call(
+    panel, mom, final, second_out = pl.pallas_call(
         functools.partial(kernel, nz, ny, nt, n_chunks, float(cols * nt)),
         out_shape=(
-            jax.ShapeDtypeStruct((rows, cols), BF16),
-            jax.ShapeDtypeStruct((rows, cols), F32),
+            jax.ShapeDtypeStruct((n_chunks, rows, width), BF16),
+            jax.ShapeDtypeStruct((n_chunks, rows, width), F32),
+            jax.ShapeDtypeStruct((rows, rows), F32),
             jax.ShapeDtypeStruct((1, rows), F32),
         ),
         in_specs=[anywhere, anywhere, anywhere, vmem],
-        out_specs=(anywhere, anywhere, vmem),
+        out_specs=(vmem, vmem, vmem, vmem),
         scratch_shapes=[
             pltpu.VMEM((n_chunks, ny * tokens, width), BF16),
             pltpu.VMEM((ny, nz, tokens, rows), BF16),
@@ -286,13 +323,11 @@
             pltpu.VMEM(hops + (rows, width), BF16),
             pltpu.VMEM(hops + (rows, width), BF16),
             pltpu.VMEM(hops + (rows, width), BF16),
-            pltpu.VMEM((n_chunks, rows, width), F32),
-            pltpu.VMEM((n_chunks, rows, width), BF16),
             pltpu.VMEM((rows, rows), F32),
             pltpu.VMEM((2, rows, width), F32),
             pltpu.VMEM((nt, rows + 8, rows), F32),
             dma((ny, n_chunks)),
-            dma((ny,)),
+            dma((ny, nz)),
             dma((max(ny - 1, 1),)),
             dma((max(ny - 1, 1),)),
             dma(hops),
@@ -300,16 +335,27 @@
             dma((nz - 1,)),
             dma((nz - 1,)),
             dma,
-            dma,
-            dma,
             dma((max(nt - 1, 1),)),
             dma((nt,)),
         ],
         compiler_params=pltpu.CompilerParams(
-            collective_id=0, has_side_effects=True, vmem_limit_bytes=60 * 1024 * 1024
+            collective_id=0, has_side_effects=True, vmem_limit_bytes=47 * 1024 * 1024
         ),
         name="normuon",
     )(out_grad, hidden, momentum, second.reshape(1, rows))
+    update, momentum_out, second_out = pl.pallas_call(
+        functools.partial(write_kernel, n_chunks),
+        out_shape=(
+            jax.ShapeDtypeStruct((rows, cols), BF16),
+            jax.ShapeDtypeStruct((rows, cols), F32),
+            jax.ShapeDtypeStruct((1, rows), F32),
+        ),
+        in_specs=[vmem] * 4,
+        out_specs=(anywhere, anywhere, vmem),
+        scratch_shapes=[pltpu.VMEM((n_chunks, rows, width), BF16), dma, dma],
+        compiler_params=pltpu.CompilerParams(vmem_limit_bytes=16 * 1024 * 1024),
+        name="write_results",
+    )(panel, mom, final, second_out)
     return update, momentum_out, second_out.reshape(rows)
 
 

time: 161 us -> 155 us (0.963)
  local copies, waits for them, and re-layouts: 5.35 us -> 1.69 us
  Pallas kernels: 155 us -> 152 us
    pallas_call x1, Pallas kernels: 155 us -> 146 us  [body(): pl.pallas_call(functools.partial(kernel, nz, ny, nt, n_chunks, float(cols...]
    pallas_call x0 -> x1, Pallas kernels: none -> 6.11 us  [body(): pl.pallas_call(functools.partial(write_kernel, n_chunks), out_shape=(jax....]
    unnamed x7 -> x4, local copies, waits for them, and re-layouts: 5.35 us -> 1.69 us
where the time goes in v2:
time: 155 us
  Pallas kernels  152 us (98%)
  local copies, waits for them, and re-layouts  1.69 us (1%)
    pallas_call x1, Pallas kernels, body(): pl.pallas_call(functools.partial(kernel, nz, ny, nt, n_chunks, float(cols...  146 us
    pallas_call x1, Pallas kernels, body(): pl.pallas_call(functools.partial(write_kernel, n_chunks), out_shape=(jax....  6.11 us

profile of v2, /device:TPU:1, one launch (start us, length us, event | category | flops | bytes accessed | tf_op | source)
XLA Modules:
  0.0 154.6 jit_solution(18349574715474287488)
XLA Ops:
  0.6 0.0 copy-start
  0.6 1.0 copy-done
  1.7 0.0 copy-start.1
  1.7 0.7 copy-done.1
  2.3 146.2 %normuon.1 = (bf16[28,128,256]{2,1,0:T(8,128)(2,1)S(1)}, f32[28,128,256]{2,1,0:T(8,128)S(1)}, f32[128,128]{1,0:T(8,128)S(1)}, f32[1,128]{1,0:T(1,128)S(1)}) custom-call(bf16[256,1024]{1,0:T(8,128)(2,1)S(1)} %copy-done, bf16[256,7168]{1,0:T(8,128)(2,1)} %h_hbm.1, f32[128,7168]{1,0:T(8,128)} %mom_hbm.1, f32[1,128]{1,0:T(1,128)S(1)} %bitcast.2), custom_call_target="tpu_custom_call" | custom-call | tf_op jit(solution)/shard_map/normuon/pallas_call | solution.py:308
  148.5 6.1 %write_results.1 = (bf16[128,7168]{1,0:T(8,128)(2,1)}, f32[128,7168]{1,0:T(8,128)}, f32[1,128]{1,0:T(1,128)}) custom-call(bf16[28,128,256]{2,1,0:T(8,128)(2,1)S(1)} %get-tuple-element.10.x, f32[28,128,256]{2,1,0:T(8,128)S(1)} %get-tuple-element.11.mom, f32[128,128]{1,0:T(8,128)S(1)} %get-tuple-element.12.final_ref, f32[1,128]{1,0:T(1,128)S(1)} %get-tuple-element.13.sec_ref), custom_call_target="tpu_custom_call" | custom-call | tf_op jit(solution)/shard_map/write_results/pallas_call | solution.py:346
Async XLA Ops:
  0.6 1.0 copy-start
  1.7 0.7 copy-start.1
